TPU v7x, 128 devices: a whole 4x4x4 slice. The times are simulated.
128 devices in a mesh: depth: 2 (over core), row: 16 (over z, x), col: 4 (over y).
Axes of the slice: x: 4, y: 4, z: 4, core: 2. Of those that a mesh axis runs over, the one named last changes fastest.
Arguments:
- right_side: bfloat16 [4, 16, 8, 128, 512], P(None, 'row', ('depth', 'col')), may hold values from -6 to 6
- inverse_diag: bfloat16 [4, 16, 8, 1, 128, 128], P(None, 'row', ('depth', 'col')), may hold values from -2 to 2.5, as said below
- coupling: bfloat16 [3, 16, 1024, 8, 2048], P(None, 'row', None, ('depth', 'col')), may hold values from -0.0625 to 0.0625
- pattern: int32 [3, 16, 8, 8, 16], P(None, 'row', None, ('depth', 'col')), may hold values 0 or 1
Outputs:
- forward_solution: bfloat16 [4, 16, 8, 128, 512], P(None, 'row', ('depth', 'col'))
- solution: bfloat16 [4, 16, 8, 128, 512], P(None, 'row', ('depth', 'col'))
Inputs may be any that keep to these rules, and one draw needn't show every extreme that they name: `inverse_diag`: each block is lower triangular with positive diagonal.
All inputs are finite; a program needn't handle non-finite values. No bound on the sum of `pattern` on one device may be relied on, other than what follows from the above.
Results may differ from a plain program's by a relative error of at most 0.025.
Values may be sent and summed in bfloat16 or wider, within the bound.
A program may use at most 128 MiB of HBM per device.

v0:
```python
import jax
import jax.numpy as jnp
from jax import lax
from jax.sharding import PartitionSpec as P


def apply_inverse(inverse, vector, transposed):
    blocks_in = vector.reshape(inverse.shape[0], inverse.shape[1], vector.shape[-1])
    einsum_form = "tji,tjn->tin" if transposed else "tij,tjn->tin"
    result = jnp.einsum(einsum_form, inverse, blocks_in, preferred_element_type=jnp.float32)
    return result.astype(jnp.bfloat16).reshape(vector.shape)


def lift_upward(masked, share_in):
    portion = lax.all_gather(share_in, "row", axis=0, tiled=True)
    span_rows = portion.shape[0] * portion.shape[2]
    return jnp.dot(
        masked, portion.reshape(span_rows, portion.shape[-1]), preferred_element_type=jnp.float32
    )


def carry_downward(masked, share_in):
    portion = lax.all_gather(share_in, ("depth", "col"), axis=1, tiled=True)
    span_rows = portion.shape[1] * portion.shape[2]
    return lax.dot_general(
        masked,
        portion.reshape(span_rows, portion.shape[-1]),
        (((0,), (0,)), ((), ())),
        preferred_element_type=jnp.float32,
    )


def forward_sum(partial_value, share_rows):
    blocks = partial_value.reshape(
        lax.axis_size(("depth", "col")), share_rows, partial_value.shape[-1]
    )
    summed = lax.psum(blocks.astype(jnp.bfloat16), ("depth", "col")).astype(jnp.float32)
    return lax.dynamic_index_in_dim(summed, lax.axis_index(("depth", "col")), 0, keepdims=False)


def backward_sum(partial_value, share_rows):
    blocks = partial_value.reshape(lax.axis_size("row"), share_rows, partial_value.shape[-1])
    summed = lax.psum(blocks.astype(jnp.bfloat16), "row").astype(jnp.float32)
    return lax.dynamic_index_in_dim(summed, lax.axis_index("row"), 0, keepdims=False)


def body(right_side, inverse_diag, coupling, pattern):
    levels = right_side.shape[0]
    share_rows = right_side.shape[3]
    rhs_cols = right_side.shape[4]
    block_width = inverse_diag.shape[-1]
    masked = []
    for pair_at in range(levels - 1):
        slab = coupling[pair_at, 0, :, 0, :]
        gate = pattern[pair_at, 0, :, 0, :].astype(jnp.bfloat16)
        shaped = (
            slab.reshape(gate.shape[0], block_width, gate.shape[1], block_width)
            * gate[:, None, :, None]
        )
        masked.append(shaped.reshape(slab.shape))
    panel_spans = [(0, rhs_cols)]
    fwd_levels = []
    for level_at in range(levels):
        pieces = []
        for panel_at, (col_first, col_last) in enumerate(panel_spans):
            source = right_side[level_at, 0, 0, :, col_first:col_last]
            if level_at == 0:
                residual = source
            else:
                partial_value = lift_upward(
                    masked[level_at - 1], fwd_levels[level_at - 1][panel_at][None, None]
                )
                residual = (
                    source.astype(jnp.float32) - forward_sum(partial_value, share_rows)
                ).astype(jnp.bfloat16)
            pieces.append(apply_inverse(inverse_diag[level_at, 0, 0], residual, False))
        fwd_levels.append(pieces)
    bwd_levels = [None] * levels
    for level_at in reversed(range(levels)):
        pieces = []
        panel_at = 0
        known_part = fwd_levels[level_at][panel_at]
        if level_at == levels - 1:
            residual = known_part
        else:
            partial_value = carry_downward(
                masked[level_at], bwd_levels[level_at + 1][panel_at][None, None]
            )
            residual = (
                known_part.astype(jnp.float32) - backward_sum(partial_value, share_rows)
            ).astype(jnp.bfloat16)
        pieces.append(apply_inverse(inverse_diag[level_at, 0, 0], residual, True))
        bwd_levels[level_at] = pieces
    forward_rows = []
    backward_rows = []
    for level_at in range(levels):
        forward_rows.append(jnp.concatenate(fwd_levels[level_at], axis=1))
        backward_rows.append(jnp.concatenate(bwd_levels[level_at], axis=1))
    forward_solution = jnp.stack(forward_rows).reshape(levels, 1, 1, share_rows, rhs_cols)
    solution = jnp.stack(backward_rows).reshape(levels, 1, 1, share_rows, rhs_cols)
    return (forward_solution, solution)


def solution(mesh):
    placed = (
        P(None, "row", ("depth", "col"), None, None),
        P(None, "row", ("depth", "col"), None, None, None),
        P(None, "row", None, ("depth", "col"), None),
        P(None, "row", None, ("depth", "col"), None),
    )
    return jax.shard_map(
        body,
        mesh=mesh,
        in_specs=placed,
        out_specs=(
            P(None, "row", ("depth", "col"), None, None),
            P(None, "row", ("depth", "col"), None, None),
        ),
        check_vma=False,
    )
```

profile of v0, /device:TPU:0, one launch (start us, length us, event | category | flops | bytes accessed | tf_op | source)
XLA Modules:
  0.0 735.9 jit_solution(18099699853977080136)
XLA Ops:
  7.2 1.8 convolution_convert_fusion.10
  9.0 0.7 convert.11
  9.8 2.6 mul.62
  12.3 7.3 mul.63
  19.6 2.6 mul.71
  22.2 7.3 mul.72
  29.6 2.6 mul.67
  32.2 7.4 mul.68
  39.5 13.6 %slice_multiply_fusion.2 = (bf16[1,1,1024,1,2048]{4,2,3,1,0:T(8,128)(2,1)}, bf16[1,1,1024,1,2048]{4,2,3,1,0:T(8,128)(2,1)}, bf16[1,1,1024,1,2048]{4,2,3,1,0:T(8,128)(2,1)}) fusion(bf16[1,1,1024,1,2048]{4,2,3,1,0:T(8,128)(2,1)} %mul.63, bf16[3,1,1024,1,2048]{4,2,3,1,0:T(8,128)(2,1)} %param.6, bf16[1,1,1024,1,2048]{4,2,3,1,0:T(8,128)(2,1)} %mul.72, ...), kind=kLoop, calls=%fused_computation.8 | loop fusion | flops 6291456 | bytes 37748736 | tf_op jit(solution)/shard_map/mul | solution.py:57
  53.1 5.1 all-gather.13.cloned.1.call-done
  58.2 6.2 fusion.9
  64.5 62.1 %all-reduce.7.cloned.1.call-done = bf16[8,128,512]{2,1,0:T(8,128)(2,1)} async-done(((bf16[8,128,512]{2,1,0:T(8,128)(2,1)}), bf16[8,128,512]{2,1,0:T(8,128)(2,1)}) %all-reduce.7.cloned.1.call-update) | async-done | bytes 1048592 | tf_op jit(solution)/shard_map/psum | solution.py:37
  126.6 1.7 convolution_convert_fusion.5
  128.4 0.0 all-reduce.9.cloned.1.call-start
  128.5 45.3 %all-gather.15.cloned.1.call-done = bf16[2048,512]{1,0:T(8,128)(2,1)} async-done(((bf16[128,512]{1,0:T(8,128)(2,1)}), bf16[2048,512]{1,0:T(8,128)(2,1)}) %all-gather.15.cloned.1.call-update) | async-done | bytes 2097168 | tf_op jit(solution)/shard_map/all_gather | solution.py:15
  173.7 6.2 fusion.12
  180.0 0.0 all-gather.17.cloned.1.call-start
  180.0 62.1 %all-reduce.9.cloned.1.call-done = bf16[8,128,512]{2,1,0:T(8,128)(2,1)} async-done(((bf16[8,128,512]{2,1,0:T(8,128)(2,1)}), bf16[8,128,512]{2,1,0:T(8,128)(2,1)}) %all-reduce.9.cloned.1.call-update) | async-done | bytes 1048592 | tf_op jit(solution)/shard_map/psum | solution.py:37
  242.1 1.7 convolution_convert_fusion.4
  243.9 0.0 all-reduce.11.cloned.1.call-start
  243.9 44.5 %all-gather.17.cloned.1.call-done = bf16[2048,512]{1,0:T(8,128)(2,1)} async-done(((bf16[128,512]{1,0:T(8,128)(2,1)}), bf16[2048,512]{1,0:T(8,128)(2,1)}) %all-gather.17.cloned.1.call-update) | async-done | bytes 2097168 | tf_op jit(solution)/shard_map/all_gather | solution.py:15
  288.5 6.2 fusion.15
  294.7 0.0 all-gather.19.cloned.1.call-start
  294.7 62.1 %all-reduce.11.cloned.1.call-done = bf16[8,128,512]{2,1,0:T(8,128)(2,1)} async-done(((bf16[8,128,512]{2,1,0:T(8,128)(2,1)}), bf16[8,128,512]{2,1,0:T(8,128)(2,1)}) %all-reduce.11.cloned.1.call-update) | async-done | bytes 1048592 | tf_op jit(solution)/shard_map/psum | solution.py:37
  356.8 1.1 convolution_convert_fusion.3
  357.9 0.9 convolution_convert_fusion.9
  358.8 0.2 all-reduce.13.cloned.1.call-start
  359.0 15.1 %fusion.2 = (bf16[2048,1024]{0,1:T(8,128)(2,1)}, bf16[2048,1024]{0,1:T(8,128)(2,1)}, bf16[2048,1024]{0,1:T(8,128)(2,1)}) fusion(bf16[128,8,16,128]{3,2,1,0:T(8,128)(2,1)} %bitcast.180, bf16[3,1,1024,1,2048]{4,2,3,1,0:T(8,128)(2,1)} %param.6, bf16[128,8,16,128]{3,2,1,0:T(8,128)(2,1)} %bitcast.182, bf16[128,8,16,128]{3,2,1,0:T(8,128)(2,1)} %bitcast.181), kind=kLoop, calls=%fused_computation.5 | loop fusion | flops 6291456 | bytes 37748736 | tf_op jit(solution)/shard_map/dot_general | solution.py:25
  374.1 6.4 copy.26
  380.5 1.1 all-gather.19.cloned.1.call-done
  381.6 6.3 convolution_convert_fusion.2
  387.9 92.3 %all-reduce.13.cloned.1.call-done = bf16[16,128,512]{2,1,0:T(8,128)(2,1)} async-done(((bf16[16,128,512]{2,1,0:T(8,128)(2,1)}), bf16[16,128,512]{2,1,0:T(8,128)(2,1)}) %all-reduce.13.cloned.1.call-update) | async-done | bytes 2097168 | tf_op jit(solution)/shard_map/psum | solution.py:43
  480.2 1.8 convolution_convert_fusion.8
  482.0 0.0 all-reduce.15.cloned.1.call-start
  482.1 6.4 copy.25
  488.5 16.4 %all-gather.21.cloned.1.call-done = bf16[1024,512]{0,1:T(8,128)(2,1)} async-done(((bf16[128,512]{0,1:T(8,128)(2,1)}), bf16[1024,512]{0,1:T(8,128)(2,1)}) %all-gather.21.cloned.1.call-update) | async-done | bytes 1048592 | tf_op jit(solution)/shard_map/all_gather | solution.py:23
  504.9 6.3 convolution_convert_fusion.1
  511.2 92.3 %all-reduce.15.cloned.1.call-done = bf16[16,128,512]{2,1,0:T(8,128)(2,1)} async-done(((bf16[16,128,512]{2,1,0:T(8,128)(2,1)}), bf16[16,128,512]{2,1,0:T(8,128)(2,1)}) %all-reduce.15.cloned.1.call-update) | async-done | bytes 2097168 | tf_op jit(solution)/shard_map/psum | solution.py:43
  603.5 1.8 convolution_convert_fusion.7
  605.3 0.0 all-reduce.17.cloned.1.call-start
  605.3 6.4 copy.24
  611.7 16.4 %all-gather.23.cloned.1.call-done = bf16[1024,512]{0,1:T(8,128)(2,1)} async-done(((bf16[128,512]{0,1:T(8,128)(2,1)}), bf16[1024,512]{0,1:T(8,128)(2,1)}) %all-gather.23.cloned.1.call-update) | async-done | bytes 1048592 | tf_op jit(solution)/shard_map/all_gather | solution.py:23
  628.2 6.3 convolution_convert_fusion
  634.5 0.9 maximum_bitcast_fusion
  635.3 91.5 %all-reduce.17.cloned.1.call-done = bf16[16,128,512]{2,1,0:T(8,128)(2,1)} async-done(((bf16[16,128,512]{2,1,0:T(8,128)(2,1)}), bf16[16,128,512]{2,1,0:T(8,128)(2,1)}) %all-reduce.17.cloned.1.call-update) | async-done | bytes 2097168 | tf_op jit(solution)/shard_map/psum | solution.py:43
  726.8 1.1 fusion.18
  728.0 0.1 maximum_bitcast_fusion.1
  728.1 1.0 copy.17
  (34 shorter events, 0.4 us)
Async XLA Ops:
  7.2 51.1 %all-gather.13.cloned.1.call-start = ((), (), s32[]{:S(2)}) async-start(), calls=%async_computation.6 | async-start | bytes 2228224 | tf_op jit(solution)/shard_map/all_gather | solution.py:15
  9.0 117.6 %all-reduce.7.cloned.1.call-start = ((), (), s32[]{:S(2)}) async-start(), calls=%async_computation | async-start | bytes 2097152 | tf_op jit(solution)/shard_map/psum | solution.py:37
  58.2 68.4 %copy-start.6 = (bf16[4,1,1,128,512]{4,3,2,1,0:T(8,128)(2,1)S(1)}, bf16[4,1,1,128,512]{4,3,2,1,0:T(8,128)(2,1)}, u32[]{:S(2)}) copy-start(bf16[4,1,1,128,512]{4,3,2,1,0:T(8,128)(2,1)} %param.4) | copy-start | bytes 1572868
  58.2 68.4 %copy-start.7 = (bf16[4,1,1,1,128,128]{5,4,3,2,1,0:T(8,128)(2,1)S(1)}, bf16[4,1,1,1,128,128]{5,4,3,2,1,0:T(8,128)(2,1)}, u32[]{:S(2)}) copy-start(bf16[4,1,1,1,128,128]{5,4,3,2,1,0:T(8,128)(2,1)} %param.5) | copy-start | bytes 393220
  64.5 109.2 %all-gather.15.cloned.1.call-start = ((), (), s32[]{:S(2)}) async-start(), calls=%async_computation.7 | async-start | bytes 2228224 | tf_op jit(solution)/shard_map/all_gather | solution.py:15
  128.4 113.7 %all-reduce.9.cloned.1.call-start = ((), (), s32[]{:S(2)}) async-start(), calls=%async_computation.1 | async-start | bytes 2097152 | tf_op jit(solution)/shard_map/psum | solution.py:37
  180.0 108.5 %all-gather.17.cloned.1.call-start = ((), (), s32[]{:S(2)}) async-start(), calls=%async_computation.8 | async-start | bytes 2228224 | tf_op jit(solution)/shard_map/all_gather | solution.py:15
  243.9 113.0 %all-reduce.11.cloned.1.call-start = ((), (), s32[]{:S(2)}) async-start(), calls=%async_computation.2 | async-start | bytes 2097152 | tf_op jit(solution)/shard_map/psum | solution.py:37
  294.7 86.9 %all-gather.19.cloned.1.call-start = ((), (), s32[]{:S(2)}) async-start(), calls=%async_computation.9 | async-start | bytes 1179648 | tf_op jit(solution)/shard_map/all_gather | solution.py:23
  358.8 121.4 %all-reduce.13.cloned.1.call-start = ((), (), s32[]{:S(2)}) async-start(), calls=%async_computation.3 | async-start | bytes 4194304 | tf_op jit(solution)/shard_map/psum | solution.py:43
  381.6 98.7 %copy-start.2 = (bf16[512,128]{0,1:T(8,128)(2,1)S(1)}, bf16[512,128]{0,1:T(8,128)(2,1)}, u32[]{:S(2)}) copy-start(bf16[512,128]{0,1:T(8,128)(2,1)} %convolution_convert_fusion.4) | copy-start | bytes 393220
  387.9 117.0 %all-gather.21.cloned.1.call-start = ((), (), s32[]{:S(2)}) async-start(), calls=%async_computation.10 | async-start | bytes 1179648 | tf_op jit(solution)/shard_map/all_gather | solution.py:23
  482.0 121.4 %all-reduce.15.cloned.1.call-start = ((), (), s32[]{:S(2)}) async-start(), calls=%async_computation.4 | async-start | bytes 4194304 | tf_op jit(solution)/shard_map/psum | solution.py:43
  504.9 98.6 %copy-start.1 = (bf16[512,128]{0,1:T(8,128)(2,1)S(1)}, bf16[512,128]{0,1:T(8,128)(2,1)}, u32[]{:S(2)}) copy-start(bf16[512,128]{0,1:T(8,128)(2,1)} %convolution_convert_fusion.5) | copy-start | bytes 393220
  511.2 117.0 %all-gather.23.cloned.1.call-start = ((), (), s32[]{:S(2)}) async-start(), calls=%async_computation.11 | async-start | bytes 1179648 | tf_op jit(solution)/shard_map/all_gather | solution.py:23
  605.3 121.5 %all-reduce.17.cloned.1.call-start = ((), (), s32[]{:S(2)}) async-start(), calls=%async_computation.5 | async-start | bytes 4194304 | tf_op jit(solution)/shard_map/psum | solution.py:43
  628.1 6.3 copy-start
  628.1 99.8 %copy-start.3 = (bf16[512,128]{1,0:T(8,128)(2,1)S(1)}, bf16[512,128]{1,0:T(8,128)(2,1)}, u32[]{:S(2)}) copy-start(bf16[512,128]{1,0:T(8,128)(2,1)} %convolution_convert_fusion.9) | copy-start | bytes 393220
  628.1 99.8 %copy-start.4 = (bf16[512,128]{1,0:T(8,128)(2,1)S(1)}, bf16[512,128]{1,0:T(8,128)(2,1)}, u32[]{:S(2)}) copy-start(bf16[512,128]{1,0:T(8,128)(2,1)} %convolution_convert_fusion.8) | copy-start | bytes 393220
  628.2 99.8 %copy-start.5 = (bf16[512,128]{1,0:T(8,128)(2,1)S(1)}, bf16[512,128]{1,0:T(8,128)(2,1)}, u32[]{:S(2)}) copy-start(bf16[512,128]{1,0:T(8,128)(2,1)} %convolution_convert_fusion.7) | copy-start | bytes 393220
Sparse Core Ops, SparseCore 0:
  10.7 47.4 all-gather.12
  64.6 61.9 all-reduce.6
  129.4 44.3 all-gather.14
  180.1 61.9 all-reduce.8
  244.1 44.3 all-gather.16
  294.8 61.9 all-reduce.10
  358.9 22.6 all-gather.18
  388.0 92.1 all-reduce.12
  482.2 22.6 all-gather.20
  511.3 92.1 all-reduce.14
  605.4 22.6 all-gather.22
  634.6 92.1 all-reduce.16
where the time goes:
time: 737 us; the launch traced here: 736 us
  waiting for transfers between devices  591 us (80%)
  local copies, waits for them, and re-layouts  50 us (7%)
  matrix products  49.3 us (7%)
  other arithmetic  30.3 us (4%)
  between operations  14.3 us (2%)
    psum x3, waiting for transfers between devices, backward_sum(): summed = lax.psum(blocks.astype(jnp.bfloat16), 'row').astype(jnp.float32)  276 us
    psum x3, waiting for transfers between devices, forward_sum(): lax.psum(blocks.astype(jnp.bfloat16), ('depth', 'col')).astype(jnp.float32)  186 us
    all_gather x3, waiting for transfers between devices, lift_upward(): portion = lax.all_gather(share_in, 'row', axis=0, tiled=True)  94.9 us
    all_gather x3, waiting for transfers between devices, carry_downward(): portion = lax.all_gather(share_in, ('depth', 'col'), axis=1, tiled=True)  33.9 us
    mul x6, local copies, waits for them, and re-layouts, body(): slab.reshape(gate.shape[0], block_width, gate.shape[1], block_width)  29.7 us
    dot_general x3, local copies, waits for them, and re-layouts, carry_downward(): lax.dot_general(masked, portion.reshape(span_rows, portion.shape[-1]), ((...  19.2 us
    dot_general x3, matrix products, carry_downward(): lax.dot_general(masked, portion.reshape(span_rows, portion.shape[-1]), ((...  18.8 us
    dot_general x3, matrix products, lift_upward(): jnp.dot(masked, portion.reshape(span_rows, portion.shape[-1]), preferred_...  18.6 us
  transfers between devices with their start and end apart: 12, of which 12 were waited for; matrix products, arithmetic and copies ran while one was open for 11% of the time, Pallas kernels for 0%

commit v1 on v0

--- a/solution.py
+++ b/solution.py
@@ -34,7 +34,7 @@
     blocks = partial_value.reshape(
         lax.axis_size(("depth", "col")), share_rows, partial_value.shape[-1]
     )
-    summed = lax.psum(blocks.astype(jnp.bfloat16), ("depth", "col")).astype(jnp.float32)
+    summed = lax.psum(lax.psum(blocks.astype(jnp.bfloat16), "col"), "depth").astype(jnp.float32)
     return lax.dynamic_index_in_dim(summed, lax.axis_index(("depth", "col")), 0, keepdims=False)
 
 

time: 737 us -> 778 us (1.056)
  waiting for transfers between devices: 591 us -> 632 us
    psum x3 -> x6, waiting for transfers between devices: 186 us -> 221 us  [the longest x3 136 us: forward_sum(): lax.psum(blocks.astype(jnp.bfloat16), 'col')]
  transfers between devices with their start and end apart: 12 -> 15, of which waited for: 12 -> 15; matrix products, arithmetic and copies ran while one was open for 11% -> 10% of each run, Pallas kernels for 0% -> 0%
where the time goes in v1:
time: 778 us; the launch traced here: 777 us
  waiting for transfers between devices  632 us (81%)
  local copies, waits for them, and re-layouts  50 us (6%)
  matrix products  49.3 us (6%)
  other arithmetic  30.3 us (4%)
  between operations  14 us (2%)
    psum x3, waiting for transfers between devices, backward_sum(): summed = lax.psum(blocks.astype(jnp.bfloat16), 'row').astype(jnp.float32)  276 us
    psum x3, waiting for transfers between devices, forward_sum(): lax.psum(blocks.astype(jnp.bfloat16), 'col')  136 us
    all_gather x3, waiting for transfers between devices, lift_upward(): portion = lax.all_gather(share_in, 'row', axis=0, tiled=True)  99 us
    psum x3, waiting for transfers between devices, forward_sum(): lax.psum(lax.psum(blocks.astype(jnp.bfloat16), 'col'), 'depth')  84.8 us
    all_gather x3, waiting for transfers between devices, carry_downward(): portion = lax.all_gather(share_in, ('depth', 'col'), axis=1, tiled=True)  36 us
    mul x6, local copies, waits for them, and re-layouts, body(): slab.reshape(gate.shape[0], block_width, gate.shape[1], block_width)  29.7 us
    dot_general x3, local copies, waits for them, and re-layouts, carry_downward(): lax.dot_general(masked, portion.reshape(span_rows, portion.shape[-1]), ((...  19.2 us
    dot_general x3, matrix products, carry_downward(): lax.dot_general(masked, portion.reshape(span_rows, portion.shape[-1]), ((...  18.8 us
  transfers between devices with their start and end apart: 15, of which 15 were waited for; matrix products, arithmetic and copies ran while one was open for 10% of the time, Pallas kernels for 0%

profile of v1, /device:TPU:0, one launch (start us, length us, event | category | flops | bytes accessed | tf_op | source)
XLA Modules:
  0.0 776.8 jit_solution(1784368637754186958)
XLA Ops:
  7.2 1.8 convolution_convert_fusion.10
  9.0 0.7 convert.11
  9.8 2.6 mul.62
  12.3 7.3 mul.63
  19.6 2.6 mul.71
  22.2 7.3 mul.72
  29.6 2.6 mul.67
  32.2 7.4 mul.68
  39.5 13.6 %slice_multiply_fusion.2 = (bf16[1,1,1024,1,2048]{4,2,3,1,0:T(8,128)(2,1)}, bf16[1,1,1024,1,2048]{4,2,3,1,0:T(8,128)(2,1)}, bf16[1,1,1024,1,2048]{4,2,3,1,0:T(8,128)(2,1)}) fusion(bf16[1,1,1024,1,2048]{4,2,3,1,0:T(8,128)(2,1)} %mul.63, bf16[3,1,1024,1,2048]{4,2,3,1,0:T(8,128)(2,1)} %param.6, bf16[1,1,1024,1,2048]{4,2,3,1,0:T(8,128)(2,1)} %mul.72, ...), kind=kLoop, calls=%fused_computation.8 | loop fusion | flops 6291456 | bytes 37748736 | tf_op jit(solution)/shard_map/mul | solution.py:57
  53.1 5.1 all-gather.13.cloned.1.call-done
  58.2 6.2 fusion.9
  64.5 45.4 %all-reduce.10.cloned.1.call-done = bf16[8,128,512]{2,1,0:T(8,128)(2,1)} async-done(((bf16[8,128,512]{2,1,0:T(8,128)(2,1)}), bf16[8,128,512]{2,1,0:T(8,128)(2,1)}) %all-reduce.10.cloned.1.call-update) | async-done | bytes 1048592 | tf_op jit(solution)/shard_map/psum | solution.py:37
  110.0 28.3 %all-reduce.12.cloned.1.call-done = bf16[8,128,512]{2,1,0:T(8,128)(2,1)} async-done(((bf16[8,128,512]{2,1,0:T(8,128)(2,1)}), bf16[8,128,512]{2,1,0:T(8,128)(2,1)}) %all-reduce.12.cloned.1.call-update) | async-done | bytes 1048592 | tf_op jit(solution)/shard_map/psum | solution.py:37
  138.4 1.8 convolution_convert_fusion.5
  140.2 47.2 %all-gather.15.cloned.1.call-done = bf16[2048,512]{1,0:T(8,128)(2,1)} async-done(((bf16[128,512]{1,0:T(8,128)(2,1)}), bf16[2048,512]{1,0:T(8,128)(2,1)}) %all-gather.15.cloned.1.call-update) | async-done | bytes 2097168 | tf_op jit(solution)/shard_map/all_gather | solution.py:15
  187.4 6.2 fusion.12
  193.6 45.4 %all-reduce.14.cloned.1.call-done = bf16[8,128,512]{2,1,0:T(8,128)(2,1)} async-done(((bf16[8,128,512]{2,1,0:T(8,128)(2,1)}), bf16[8,128,512]{2,1,0:T(8,128)(2,1)}) %all-reduce.14.cloned.1.call-update) | async-done | bytes 1048592 | tf_op jit(solution)/shard_map/psum | solution.py:37
  239.1 28.2 %all-reduce.16.cloned.1.call-done = bf16[8,128,512]{2,1,0:T(8,128)(2,1)} async-done(((bf16[8,128,512]{2,1,0:T(8,128)(2,1)}), bf16[8,128,512]{2,1,0:T(8,128)(2,1)}) %all-reduce.16.cloned.1.call-update) | async-done | bytes 1048592 | tf_op jit(solution)/shard_map/psum | solution.py:37
  267.3 1.7 convolution_convert_fusion.4
  269.0 0.0 all-reduce.18.cloned.1.call-start
  269.1 46.7 %all-gather.17.cloned.1.call-done = bf16[2048,512]{1,0:T(8,128)(2,1)} async-done(((bf16[128,512]{1,0:T(8,128)(2,1)}), bf16[2048,512]{1,0:T(8,128)(2,1)}) %all-gather.17.cloned.1.call-update) | async-done | bytes 2097168 | tf_op jit(solution)/shard_map/all_gather | solution.py:15
  315.8 6.2 fusion.15
  322.1 45.5 %all-reduce.18.cloned.1.call-done = bf16[8,128,512]{2,1,0:T(8,128)(2,1)} async-done(((bf16[8,128,512]{2,1,0:T(8,128)(2,1)}), bf16[8,128,512]{2,1,0:T(8,128)(2,1)}) %all-reduce.18.cloned.1.call-update) | async-done | bytes 1048592 | tf_op jit(solution)/shard_map/psum | solution.py:37
  367.6 28.3 %all-reduce.20.cloned.1.call-done = bf16[8,128,512]{2,1,0:T(8,128)(2,1)} async-done(((bf16[8,128,512]{2,1,0:T(8,128)(2,1)}), bf16[8,128,512]{2,1,0:T(8,128)(2,1)}) %all-reduce.20.cloned.1.call-update) | async-done | bytes 1048592 | tf_op jit(solution)/shard_map/psum | solution.py:37
  396.0 1.1 convolution_convert_fusion.3
  397.1 0.9 convolution_convert_fusion.9
  397.9 0.2 all-reduce.22.cloned.1.call-start
  398.2 15.0 %fusion.2 = (bf16[2048,1024]{0,1:T(8,128)(2,1)}, bf16[2048,1024]{0,1:T(8,128)(2,1)}, bf16[2048,1024]{0,1:T(8,128)(2,1)}) fusion(bf16[128,8,16,128]{3,2,1,0:T(8,128)(2,1)} %bitcast.180, bf16[3,1,1024,1,2048]{4,2,3,1,0:T(8,128)(2,1)} %param.6, bf16[128,8,16,128]{3,2,1,0:T(8,128)(2,1)} %bitcast.182, bf16[128,8,16,128]{3,2,1,0:T(8,128)(2,1)} %bitcast.181), kind=kLoop, calls=%fused_computation.5 | loop fusion | flops 6291456 | bytes 37748736 | tf_op jit(solution)/shard_map/dot_general | solution.py:25
  413.2 6.4 copy.26
  419.6 3.2 all-gather.19.cloned.1.call-done
  422.7 6.3 convolution_convert_fusion.2
  429.1 92.3 %all-reduce.22.cloned.1.call-done = bf16[16,128,512]{2,1,0:T(8,128)(2,1)} async-done(((bf16[16,128,512]{2,1,0:T(8,128)(2,1)}), bf16[16,128,512]{2,1,0:T(8,128)(2,1)}) %all-reduce.22.cloned.1.call-update) | async-done | bytes 2097168 | tf_op jit(solution)/shard_map/psum | solution.py:43
  521.4 1.8 convolution_convert_fusion.8
  523.2 0.0 all-reduce.24.cloned.1.call-start
  523.2 6.4 copy.25
  529.6 16.4 %all-gather.21.cloned.1.call-done = bf16[1024,512]{0,1:T(8,128)(2,1)} async-done(((bf16[128,512]{0,1:T(8,128)(2,1)}), bf16[1024,512]{0,1:T(8,128)(2,1)}) %all-gather.21.cloned.1.call-update) | async-done | bytes 1048592 | tf_op jit(solution)/shard_map/all_gather | solution.py:23
  546.0 6.3 convolution_convert_fusion.1
  552.3 0.0 all-gather.23.cloned.1.call-start
  552.4 92.3 %all-reduce.24.cloned.1.call-done = bf16[16,128,512]{2,1,0:T(8,128)(2,1)} async-done(((bf16[16,128,512]{2,1,0:T(8,128)(2,1)}), bf16[16,128,512]{2,1,0:T(8,128)(2,1)}) %all-reduce.24.cloned.1.call-update) | async-done | bytes 2097168 | tf_op jit(solution)/shard_map/psum | solution.py:43
  644.6 1.8 convolution_convert_fusion.7
  646.5 6.4 copy.24
  652.9 16.4 %all-gather.23.cloned.1.call-done = bf16[1024,512]{0,1:T(8,128)(2,1)} async-done(((bf16[128,512]{0,1:T(8,128)(2,1)}), bf16[1024,512]{0,1:T(8,128)(2,1)}) %all-gather.23.cloned.1.call-update) | async-done | bytes 1048592 | tf_op jit(solution)/shard_map/all_gather | solution.py:23
  669.3 6.3 convolution_convert_fusion
  675.6 0.9 maximum_bitcast_fusion
  676.5 91.5 %all-reduce.26.cloned.1.call-done = bf16[16,128,512]{2,1,0:T(8,128)(2,1)} async-done(((bf16[16,128,512]{2,1,0:T(8,128)(2,1)}), bf16[16,128,512]{2,1,0:T(8,128)(2,1)}) %all-reduce.26.cloned.1.call-update) | async-done | bytes 2097168 | tf_op jit(solution)/shard_map/psum | solution.py:43
  768.0 1.1 fusion.18
  769.1 0.1 maximum_bitcast_fusion.1
  769.2 1.0 copy.17
  (43 shorter events, 0.7 us)
Async XLA Ops:
  7.2 51.1 %all-gather.13.cloned.1.call-start = ((), (), s32[]{:S(2)}) async-start(), calls=%async_computation.9 | async-start | bytes 2228224 | tf_op jit(solution)/shard_map/all_gather | solution.py:15
  9.0 101.0 %all-reduce.10.cloned.1.call-start = ((), (), s32[]{:S(2)}) async-start(), calls=%async_computation | async-start | bytes 2097152 | tf_op jit(solution)/shard_map/psum | solution.py:37
  58.2 80.1 %copy-start.6 = (bf16[4,1,1,128,512]{4,3,2,1,0:T(8,128)(2,1)S(1)}, bf16[4,1,1,128,512]{4,3,2,1,0:T(8,128)(2,1)}, u32[]{:S(2)}) copy-start(bf16[4,1,1,128,512]{4,3,2,1,0:T(8,128)(2,1)} %param.4) | copy-start | bytes 1572868
  58.2 80.1 %copy-start.7 = (bf16[4,1,1,1,128,128]{5,4,3,2,1,0:T(8,128)(2,1)S(1)}, bf16[4,1,1,1,128,128]{5,4,3,2,1,0:T(8,128)(2,1)}, u32[]{:S(2)}) copy-start(bf16[4,1,1,1,128,128]{5,4,3,2,1,0:T(8,128)(2,1)} %param.5) | copy-start | bytes 393220
  64.5 73.9 %all-reduce.12.cloned.1.call-start = ((), (), s32[]{:S(2)}) async-start(), calls=%async_computation.1 | async-start | bytes 2097152 | tf_op jit(solution)/shard_map/psum | solution.py:37
  110.0 77.4 %all-gather.15.cloned.1.call-start = ((), (), s32[]{:S(2)}) async-start(), calls=%async_computation.10 | async-start | bytes 2228224 | tf_op jit(solution)/shard_map/all_gather | solution.py:15
  140.1 98.9 %all-reduce.14.cloned.1.call-start = ((), (), s32[]{:S(2)}) async-start(), calls=%async_computation.2 | async-start | bytes 2097152 | tf_op jit(solution)/shard_map/psum | solution.py:37
  193.6 73.7 %all-reduce.16.cloned.1.call-start = ((), (), s32[]{:S(2)}) async-start(), calls=%async_computation.3 | async-start | bytes 2097152 | tf_op jit(solution)/shard_map/psum | solution.py:37
  239.0 76.8 %all-gather.17.cloned.1.call-start = ((), (), s32[]{:S(2)}) async-start(), calls=%async_computation.11 | async-start | bytes 2228224 | tf_op jit(solution)/shard_map/all_gather | solution.py:15
  269.0 98.5 %all-reduce.18.cloned.1.call-start = ((), (), s32[]{:S(2)}) async-start(), calls=%async_computation.4 | async-start | bytes 2097152 | tf_op jit(solution)/shard_map/psum | solution.py:37
  322.0 73.9 %all-reduce.20.cloned.1.call-start = ((), (), s32[]{:S(2)}) async-start(), calls=%async_computation.5 | async-start | bytes 2097152 | tf_op jit(solution)/shard_map/psum | solution.py:37
  367.6 55.2 %all-gather.19.cloned.1.call-start = ((), (), s32[]{:S(2)}) async-start(), calls=%async_computation.12 | async-start | bytes 1179648 | tf_op jit(solution)/shard_map/all_gather | solution.py:23
  397.9 123.5 %all-reduce.22.cloned.1.call-start = ((), (), s32[]{:S(2)}) async-start(), calls=%async_computation.6 | async-start | bytes 4194304 | tf_op jit(solution)/shard_map/psum | solution.py:43
  422.7 98.7 %copy-start.2 = (bf16[512,128]{0,1:T(8,128)(2,1)S(1)}, bf16[512,128]{0,1:T(8,128)(2,1)}, u32[]{:S(2)}) copy-start(bf16[512,128]{0,1:T(8,128)(2,1)} %convolution_convert_fusion.4) | copy-start | bytes 393220
  429.0 117.0 %all-gather.21.cloned.1.call-start = ((), (), s32[]{:S(2)}) async-start(), calls=%async_computation.13 | async-start | bytes 1179648 | tf_op jit(solution)/shard_map/all_gather | solution.py:23
  523.2 121.5 %all-reduce.24.cloned.1.call-start = ((), (), s32[]{:S(2)}) async-start(), calls=%async_computation.7 | async-start | bytes 4194304 | tf_op jit(solution)/shard_map/psum | solution.py:43
  546.0 98.6 %copy-start.1 = (bf16[512,128]{0,1:T(8,128)(2,1)S(1)}, bf16[512,128]{0,1:T(8,128)(2,1)}, u32[]{:S(2)}) copy-start(bf16[512,128]{0,1:T(8,128)(2,1)} %convolution_convert_fusion.5) | copy-start | bytes 393220
  552.3 117.0 %all-gather.23.cloned.1.call-start = ((), (), s32[]{:S(2)}) async-start(), calls=%async_computation.14 | async-start | bytes 1179648 | tf_op jit(solution)/shard_map/all_gather | solution.py:23
  646.4 121.5 %all-reduce.26.cloned.1.call-start = ((), (), s32[]{:S(2)}) async-start(), calls=%async_computation.8 | async-start | bytes 4194304 | tf_op jit(solution)/shard_map/psum | solution.py:43
  669.3 6.3 copy-start
  669.3 99.8 %copy-start.3 = (bf16[512,128]{1,0:T(8,128)(2,1)S(1)}, bf16[512,128]{1,0:T(8,128)(2,1)}, u32[]{:S(2)}) copy-start(bf16[512,128]{1,0:T(8,128)(2,1)} %convolution_convert_fusion.9) | copy-start | bytes 393220
  669.3 99.8 %copy-start.4 = (bf16[512,128]{1,0:T(8,128)(2,1)S(1)}, bf16[512,128]{1,0:T(8,128)(2,1)}, u32[]{:S(2)}) copy-start(bf16[512,128]{1,0:T(8,128)(2,1)} %convolution_convert_fusion.8) | copy-start | bytes 393220
  669.3 99.8 %copy-start.5 = (bf16[512,128]{1,0:T(8,128)(2,1)S(1)}, bf16[512,128]{1,0:T(8,128)(2,1)}, u32[]{:S(2)}) copy-start(bf16[512,128]{1,0:T(8,128)(2,1)} %convolution_convert_fusion.7) | copy-start | bytes 393220
Sparse Core Ops, SparseCore 0:
  10.7 47.4 all-gather.12
  64.6 45.3 all-reduce.9
  112.4 25.8 all-reduce.11
  140.9 46.3 all-gather.14
  193.7 45.2 all-reduce.13
  241.3 25.8 all-reduce.15
  269.4 46.3 all-gather.16
  322.2 45.3 all-reduce.17
  370.0 25.8 all-reduce.19
  398.1 24.6 all-gather.18
  429.2 92.1 all-reduce.21
  523.3 22.6 all-gather.20
  552.5 92.1 all-reduce.23
  646.6 22.6 all-gather.22
  675.7 92.1 all-reduce.25
